TPU v7x, 32 devices: a whole 2x2x4 slice. The times are simulated.
32 devices in a mesh: tm: 8 (over z, x), space: 4 (over y, core).
Axes of the slice: x: 2, y: 2, z: 4, core: 2. Of those that a mesh axis runs over, the one named last changes fastest.
Arguments:
- state: float32 [32, 16, 64, 128], P('tm', 'space'), may hold values from -6 to 6
- source: float32 [32, 16, 64, 128], P('tm', 'space'), may hold values from -6 to 6
- absorption: float32 [16, 64, 128], P('space'), may hold values from 0.05 to 0.5
Outputs:
- relaxed: float32 [32, 16, 64, 128], P('tm', 'space')
- coarse_residual: float32 [8, 16, 64, 128], P('tm', 'space')
- residual_norm: float32 [], replicated
All inputs are finite; a program needn't handle non-finite values.
Results may differ from a plain program's by a relative error of at most 0.0004.
Values sent between devices are 32-bit elements; how exact they have to be, the bound alone decides.
A program may use at most 64 MiB of HBM per device.

v0:
```python
import math

import jax
import jax.numpy as jnp
from jax import lax
from jax.sharding import PartitionSpec as P

CF = 4
SWEEPS = 5


coupling = 4.0


def shifted(value, axis, by):
    count = lax.axis_size(axis)
    pairs = [(i, i + by) for i in range(count) if 0 <= i + by < count]
    return lax.ppermute(value, axis, pairs)


def sweep_weights(count):
    spread = 6.0 * coupling / (1.0 + 6.0 * coupling)
    return [
        1.0 / (1.0 + spread * math.cos(math.pi * (2 * k + 1) / (2 * count))) for k in range(count)
    ]


def apply_inner(extended, diag):
    inner = extended[1:-1]
    sides = jnp.pad(inner, ((0, 0), (1, 1), (1, 1)))
    beside = extended[2:] + extended[:-2]
    beside = beside + sides[:, 2:, 1:-1] + sides[:, :-2, 1:-1]
    beside = beside + sides[:, 1:-1, 2:] + sides[:, 1:-1, :-2]
    return diag * inner - coupling * beside


def step_whole(rhs, diag_full):
    field = rhs / diag_full
    for weight in sweep_weights(SWEEPS):
        extended = jnp.pad(field, ((1, 1), (0, 0), (0, 0)))
        field = field + weight * (rhs - apply_inner(extended, diag_full)) / diag_full
    return field


def local(state, source, absorption):
    depth_cells = absorption.shape[0]
    offset = lax.axis_index("space") * depth_cells

    def previous(last):
        return shifted(last, "tm", 1)

    stacked = jnp.concatenate([state[:1], source, absorption[None]], axis=0)
    gathered = lax.all_gather(stacked, "space", axis=1, tiled=True)
    source_full = gathered[1 : CF + 1]
    diag_full = 1.0 + 6.0 * coupling + gathered[CF + 1]

    def own_layers(field):
        return lax.dynamic_slice_in_dim(field, offset, depth_cells, 0)

    def back_full(last):
        return lax.all_gather(previous(own_layers(last)), "space", axis=0, tiled=True)

    points = [gathered[0]] + [None] * (CF - 1)

    def relax_full(points):
        for j in range(1, CF):
            points[j] = step_whole(points[j - 1], diag_full) + source_full[j]
        return points

    points = relax_full(points)
    points[0] = step_whole(back_full(points[-1]), diag_full) + source_full[0]
    points = relax_full(points)
    coarse_full = source_full[0] + step_whole(back_full(points[-1]), diag_full) - points[0]
    coarse_residual = own_layers(coarse_full)
    points = [own_layers(point) for point in points]
    residual_norm = lax.psum(jnp.sum(coarse_residual * coarse_residual), ("tm", "space"))
    relaxed = jnp.stack(points, axis=0)
    return (relaxed, coarse_residual[None], residual_norm)


def solution(mesh):
    return jax.shard_map(
        local,
        mesh=mesh,
        in_specs=(
            P("tm", "space", None, None),
            P("tm", "space", None, None),
            P("space", None, None),
        ),
        out_specs=(P("tm", "space", None, None), P("tm", "space", None, None), P()),
        check_vma=False,
    )
```

profile of v0, /device:TPU:0, one launch (start us, length us, event | category | flops | bytes accessed | tf_op | source)
XLA Modules:
  0.0 141.3 jit_solution(12284245266139244024)
XLA Ops:
  7.2 0.9 slice.790
  8.1 2.1 %pad_maximum_fusion = f32[6,4,64,128]{3,2,1,0:T(8,128)} fusion(f32[1,4,64,128]{3,2,1,0:T(8,128)} %bitcast.153, f32[4,4,64,128]{3,2,1,0:T(8,128)} %param.4, f32[1,4,64,128]{3,2,1,0:T(8,128)S(1)} %slice.790), kind=kLoop, calls=%fused_computation.160 | loop fusion | flops 393216 | bytes 1572864 | tf_op jit(solution)/shard_map/concatenate | solution.py:52
  10.2 31.4 %all-gather.2.cloned.1.call-done = f32[6,16,64,128]{3,2,1,0:T(8,128)} async-done(((f32[6,4,64,128]{3,2,1,0:T(8,128)}), f32[6,16,64,128]{3,2,1,0:T(8,128)}) %all-gather.2.cloned.1.call-update) | async-done | bytes 3145744 | tf_op jit(solution)/shard_map/all_gather | solution.py:53
  41.6 1.4 %fusion.424 = f32[16,64,128]{2,1,0:T(8,128)S(1)} fusion(f32[6,16,64,128]{3,2,1,0:T(8,128)} %all-gather.2.cloned.1.call-done), kind=kLoop, calls=%fused_computation.672 | loop fusion | flops 262144 | bytes 1572864 | tf_op jit(solution)/shard_map/div | solution.py:38
  43.1 1.6 %fusion.10 = f32[16,64,128]{2,1,0:T(8,128)S(1)} fusion(f32[16,64,128]{2,1,0:T(8,128)S(1)} %fusion.424, f32[6,16,64,128]{3,2,1,0:T(8,128)} %all-gather.2.cloned.1.call-done), kind=kLoop, calls=%fused_computation.251 | loop fusion | flops 1703936 | bytes 2097152 | tf_op jit(solution)/shard_map/add | solution.py:41
  46.0 0.4 fusion.443
  47.3 0.4 fusion.86
  48.2 0.4 fusion.441
  50.0 0.5 fusion.439
  51.1 3.4 %collective-permute-start = (f32[4,64,128]{2,1,0:T(8,128)S(1)}, f32[4,64,128]{2,1,0:T(8,128)S(1)}, u32[]{:S(2)}, u32[]{:S(2)}) collective-permute-start(f32[4,64,128]{2,1,0:T(8,128)S(1)} %fusion.432), channel_id=1, source_target_pairs={{0,4},{4,8},{8,12},{12,16},{16,20},{20,24},{24,28},{1,5},{5,9},{9,... | collective-permute-start | bytes 393224 | tf_op jit(solution)/shard_map/ppermute | solution.py:18
  54.5 3.1 %collective-permute-done = f32[4,64,128]{2,1,0:T(8,128)S(1)} collective-permute-done((f32[4,64,128]{2,1,0:T(8,128)S(1)}, f32[4,64,128]{2,1,0:T(8,128)S(1)}, u32[]{:S(2)}, u32[]{:S(2)}) %collective-permute-start) | collective-permute-done | bytes 131104 | tf_op jit(solution)/shard_map/ppermute | solution.py:18
  57.6 6.7 %all_gather.10 = f32[16,64,128]{2,1,0:T(8,128)S(1)} all-gather(f32[4,64,128]{2,1,0:T(8,128)S(1)} %collective-permute-done), channel_id=1, replica_groups=mesh['tm'=8,'space'=4] {'space'}, dimensions={0}, use_global_device_ids=true | all-gather | bytes 655360 | tf_op jit(solution)/shard_map/all_gather | solution.py:61
  65.2 0.4 fusion.190
  66.1 0.4 fusion.435
  68.3 0.4 fusion.442
  70.5 0.4 fusion.436
  72.3 0.5 fusion.440
  73.2 4.4 %collective-permute-start.1 = (f32[4,64,128]{2,1,0:T(8,128)S(1)}, f32[4,64,128]{2,1,0:T(8,128)S(1)}, u32[]{:S(2)}, u32[]{:S(2)}) collective-permute-start(f32[4,64,128]{2,1,0:T(8,128)S(1)} %get-tuple-element.24), channel_id=1, source_target_pairs={{0,4},{4,8},{8,12},{12,16},{16,20},{20,24},{24,28},{1,5},{5,9},{9,... | collective-permute-start | bytes 393224 | tf_op jit(solution)/shard_map/ppermute | solution.py:18
  77.6 3.2 %collective-permute-done.1 = f32[4,64,128]{2,1,0:T(8,128)S(1)} collective-permute-done((f32[4,64,128]{2,1,0:T(8,128)S(1)}, f32[4,64,128]{2,1,0:T(8,128)S(1)}, u32[]{:S(2)}, u32[]{:S(2)}) %collective-permute-start.1) | collective-permute-done | bytes 131104 | tf_op jit(solution)/shard_map/ppermute | solution.py:18
  80.8 6.9 %all_gather.11 = f32[16,64,128]{2,1,0:T(8,128)S(1)} all-gather(f32[4,64,128]{2,1,0:T(8,128)S(1)} %collective-permute-done.1), channel_id=1, replica_groups=mesh['tm'=8,'space'=4] {'space'}, dimensions={0}, use_global_device_ids=true | all-gather | bytes 655360 | tf_op jit(solution)/shard_map/all_gather | solution.py:61
  88.7 0.5 fusion.404
  90.0 1.3 multiply_reduce_fusion
  91.3 42.3 %psum.7 = f32[]{:T(128)} all-reduce(f32[]{:T(128)} %get-tuple-element.3), channel_id=1, replica_groups=mesh['tm'=8,'space'=4] {'tm','space'}, use_global_device_ids=true, to_apply=%region_1.2 | all-reduce | flops 1 | bytes 8 | tf_op jit(solution)/shard_map/psum | solution.py:76
  133.6 0.8 pad_maximum_fusion.1
  (39 shorter events, 12.8 us)
Async XLA Ops:
  7.2 34.5 %all-gather.2.cloned.1.call-start = ((), (), s32[]{:S(2)}) async-start(), calls=%async_computation | async-start | bytes 3932160 | tf_op jit(solution)/shard_map/all_gather | solution.py:53
  41.6 3.1 %copy-start = (f32[6,16,64,128]{3,2,1,0:T(8,128)S(1)}, f32[6,16,64,128]{3,2,1,0:T(8,128)}, u32[]{:S(2)}) copy-start(f32[6,16,64,128]{3,2,1,0:T(8,128)} %all-gather.2.cloned.1.call-done) | copy-start | bytes 9437188
  51.1 6.5 %collective-permute-start = (f32[4,64,128]{2,1,0:T(8,128)S(1)}, f32[4,64,128]{2,1,0:T(8,128)S(1)}, u32[]{:S(2)}, u32[]{:S(2)}) collective-permute-start(f32[4,64,128]{2,1,0:T(8,128)S(1)} %fusion.432), channel_id=1, source_target_pairs={{0,4},{4,8},{8,12},{12,16},{16,20},{20,24},{24,28},{1,5},{5,9},{9,... | collective-permute-start | bytes 393224 | tf_op jit(solution)/shard_map/ppermute | solution.py:18
  73.2 7.6 %collective-permute-start.1 = (f32[4,64,128]{2,1,0:T(8,128)S(1)}, f32[4,64,128]{2,1,0:T(8,128)S(1)}, u32[]{:S(2)}, u32[]{:S(2)}) collective-permute-start(f32[4,64,128]{2,1,0:T(8,128)S(1)} %get-tuple-element.24), channel_id=1, source_target_pairs={{0,4},{4,8},{8,12},{12,16},{16,20},{20,24},{24,28},{1,5},{5,9},{9,... | collective-permute-start | bytes 393224 | tf_op jit(solution)/shard_map/ppermute | solution.py:18
Sparse Core Ops, SparseCore 0:
  10.4 31.2 all-gather.1
where the time goes:
time: 142 us; the launch traced here: 141 us
  blocking collectives  55.8 us (39%)
  waiting for transfers between devices  37.7 us (27%)
  other arithmetic  24.6 us (17%)
  between operations  14.3 us (10%)
  starting transfers between devices  7.81 us (6%)
    psum x1, blocking collectives, local(): lax.psum(jnp.sum(coarse_residual * coarse_residual), ('tm', 'space'))  42.3 us
    all_gather x1, waiting for transfers between devices, local(): gathered = lax.all_gather(stacked, 'space', axis=1, tiled=True)  31.4 us
    add x30, other arithmetic, step_whole(): field + weight * (rhs - apply_inner(extended, diag_full)) / diag_full  14.2 us
    all_gather x2, blocking collectives, back_full(): lax.all_gather(previous(own_layers(last)), 'space', axis=0, tiled=True)  13.5 us
    ppermute x2, starting transfers between devices, shifted(): return lax.ppermute(value, axis, pairs)  7.77 us
    ppermute x2, waiting for transfers between devices, shifted(): return lax.ppermute(value, axis, pairs)  6.35 us
    div x8, other arithmetic, step_whole(): field = rhs / diag_full  3.89 us
  transfers between devices with their start and end apart: 3, of which 3 were waited for; matrix products, arithmetic and copies ran while one was open for 0% of the time, Pallas kernels for 0%

commit v1 on v0

v1 whole, which is shorter than its diff:
```python
import functools
import math

import jax
import jax.numpy as jnp
import numpy as np
from jax import lax
from jax.experimental import pallas as pl
from jax.experimental.pallas import tpu as pltpu
from jax.sharding import PartitionSpec as P

CF = 4
SWEEPS = 5
SUB = 8

coupling = 4.0
MESH = pl.DeviceIdType.MESH


def series():
    spread = 6.0 * coupling / (1.0 + 6.0 * coupling)
    one = np.polynomial.Polynomial([1.0])
    var = np.polynomial.Polynomial([0.0, 1.0])
    x = one
    for k in range(SWEEPS):
        weight = 1.0 / (1.0 + spread * math.cos(math.pi * (2 * k + 1) / (2 * SWEEPS)))
        x = x + weight * (one - (one - var) * x)
    c = x.coef
    return float(c[0]), float(c[2]), float(c[4])


def kernel(nt, ns, state, source, absorb, relaxed, resid, norm,
           nat, c4, work, held, full, pfull, qown, qin, tot, allsp, alltm, parts,
           loc_sem, g_send, g_recv, p_send, p_recv, sh_send, q_send, q_recv,
           n_send, n_recv):
    tm = lax.axis_index("tm")
    s = lax.axis_index("space")
    depth, rows, cols = absorb.shape
    lo = rows // SUB
    layers = ns * depth
    others = ns // 2 - 1
    partner = s + 1 - 2 * lax.rem(s, 2)
    chips = [lax.rem(s + 2 * i, ns) for i in range(1, others + 1)]
    r0, r1, r2 = series()
    own = s * depth

    barrier = pltpu.get_barrier_semaphore()
    for i in range(1, ns):
        pl.semaphore_signal(barrier, inc=1, device_id=(tm, lax.rem(s + i, ns)), device_id_type=MESH)
    for i in range(1, nt):
        pl.semaphore_signal(barrier, inc=1, device_id=(lax.rem(tm + i, nt), s), device_id_type=MESH)

    srcs = [absorb, state.at[0]] + [source.at[j] for j in range(1, CF)] + [source.at[0]]
    fields = len(srcs)
    quarter = lambda f, q: nat.at[f, pl.ds(q * depth, depth)]
    loads = [pltpu.make_async_copy(srcs[f], quarter(f, s), loc_sem.at[f]) for f in range(fields)]
    for load in loads:
        load.start()
    work[0] = jnp.zeros(work.shape[1:], jnp.float32)
    work[layers + 1] = jnp.zeros(work.shape[1:], jnp.float32)

    pl.semaphore_wait(barrier, ns - 1 + nt - 1)

    def remote(src, dst, send, recv, where):
        return pltpu.make_async_remote_copy(
            src_ref=src, dst_ref=dst, send_sem=send, recv_sem=recv,
            device_id=where, device_id_type=MESH)

    pending = []

    def go(copy):
        copy.start()
        pending.append(copy)

    for f in range(fields):
        for i, chip in enumerate(chips):
            go(remote(srcs[f], quarter(f, s), g_send.at[f, 1 + i], g_recv.at[f, s], (tm, chip)))
        go(remote(srcs[f], quarter(f, s), g_send.at[f, 0], g_recv.at[f, s], (tm, partner)))

    def relay(f):
        for i, chip in enumerate(chips):
            here = quarter(f, chip)
            remote(here, here, g_send.at[f, 0], g_recv.at[f, chip], (tm, partner)).wait_recv()
            go(remote(here, here, g_send.at[f, 1 + others + i], g_recv.at[f, chip], (tm, partner)))

    def arrive(f, mine=True):
        if mine:
            loads[f].wait()
        there = [partner] + [lax.rem(partner + 2 * i, ns) for i in range(1, others + 1)]
        for q in there:
            here = quarter(f, q)
            remote(here, here, g_send.at[f, 0], g_recv.at[f, q], (tm, partner)).wait_recv()

    def natural(f, z):
        return jnp.stack([nat[f, z, pl.ds(i, SUB, stride=lo), :] for i in range(lo)])

    lane = lax.broadcasted_iota(jnp.int32, (lo, SUB, cols), 2)
    first_lane, last_lane = lane == 0, lane == cols - 1
    sub = lax.broadcasted_iota(jnp.int32, (SUB, cols), 0)
    first_sub, last_sub = sub == 0, sub == SUB - 1

    def beside(v):
        up = jnp.where(first_sub, 0.0, pltpu.roll(v[lo - 1], 1, 0))
        down = jnp.where(last_sub, 0.0, pltpu.roll(v[0], SUB - 1, 0))
        total = jnp.concatenate([up[None], v[:-1]]) + jnp.concatenate([v[1:], down[None]])
        flat = v.reshape(lo * SUB, cols)
        left = pltpu.roll(flat, 1, 1).reshape(v.shape)
        right = pltpu.roll(flat, cols - 1, 1).reshape(v.shape)
        return total + jnp.where(first_lane, 0.0, left) + jnp.where(last_lane, 0.0, right)

    def sweep(finish, unroll=4):
        def body(i, carry):
            before, now = carry
            for j in range(unroll):
                z = i * unroll + j
                after = work[z + 2]
                finish(z, c4[z] * (before + after + beside(now)), now)
                before, now = now, after
            return before, now
        lax.fori_loop(0, layers // unroll, body, (work[0], work[1]))

    def plain(z, moved, now):
        work[z + 1] = moved

    def adding(factor):
        def finish(z, moved, now):
            work[z + 1] = moved + factor * held[z]
        return finish

    def start_with(z, value):
        h = value * (c4[z] * (r2 / coupling))
        work[z + 1] = h
        held[z] = h

    def phi(finish):
        sweep(plain)
        sweep(adding(r1 / r2))
        sweep(plain)
        sweep(adding(r0 / r2))
        sweep(finish)

    def each_layer(do):
        def body(z, _):
            do(z)
            return 0
        lax.fori_loop(0, layers, body, 0)

    def onward(f):
        def finish(z, moved, now):
            value = now + moved + natural(f, z)
            full[z] = value
            start_with(z, value)
        return finish

    def to_full(z, moved, now):
        full[z] = now + moved

    def put(ref, d, value):
        for i in range(lo):
            ref[d, pl.ds(i, SUB, stride=lo), :] = value[i]

    relay(0)
    relay(1)
    arrive(0)

    def scale(z):
        c4[z] = coupling / (1.0 + 6.0 * coupling + natural(0, z))
    each_layer(scale)
    relay(2)
    arrive(1)
    each_layer(lambda z: start_with(z, natural(1, z)))
    relay(3)
    arrive(2)
    phi(onward(2))
    relay(4)
    arrive(3)
    phi(onward(3))
    phi(to_full)
    relay(5)

    loads[4].wait()
    chunk = lambda d: pl.ds(own + d, 1)
    for d in range(depth):
        qown[0, d] = full[own + d] + natural(4, own + d)
    shifts = [remote(qown.at[0, pl.ds(d, 1)], pfull.at[chunk(d)], sh_send.at[d], p_recv.at[d, s],
                     (lax.rem(tm + 1, nt), s)) for d in range(depth)]

    @pl.when(tm < nt - 1)
    def _():
        for shift in shifts:
            shift.start()

    @pl.when(tm == 0)
    def _():
        def zero(z):
            pfull[z] = jnp.zeros(pfull.shape[1:], jnp.float32)
        each_layer(zero)

    @pl.when(tm > 0)
    def _():
        copies = []

        def send(src, send_sem, recv_sem, where):
            copy = remote(src, src, send_sem, recv_sem, where)
            copy.start()
            copies.append(copy)

        for d in range(depth):
            here = pfull.at[chunk(d)]
            shifts[d].wait_recv()
            for i, chip in enumerate(chips):
                send(here, p_send.at[d, 1 + i], p_recv.at[d, s], (tm, chip))
            send(here, p_send.at[d, 0], p_recv.at[d, s], (tm, partner))
        for d in range(depth):
            for i, chip in enumerate(chips):
                here = pfull.at[pl.ds(chip * depth + d, 1)]
                remote(here, here, p_send.at[d, 0], p_recv.at[d, chip], (tm, partner)).wait_recv()
                send(here, p_send.at[d, 1 + others + i], p_recv.at[d, chip], (tm, partner))
        for d in range(depth):
            for q in [partner] + [lax.rem(partner + 2 * i, ns) for i in range(1, others + 1)]:
                here = pfull.at[pl.ds(q * depth + d, 1)]
                remote(here, here, p_send.at[d, 0], p_recv.at[d, q], (tm, partner)).wait_recv()
        for copy in copies:
            copy.wait_send()

    @pl.when(tm < nt - 1)
    def _():
        for shift in shifts:
            shift.wait_send()

    arrive(4, mine=False)
    arrive(5)

    def save(j):
        for d in range(depth):
            put(relaxed.at[j], d, full[own + d])

    each_layer(lambda z: start_with(z, pfull[z]))
    phi(onward(5))
    save(0)
    for j in range(1, CF):
        phi(onward(1 + j))
        save(j)
    phi(to_full)
    for d in range(depth):
        qown[1, d] = full[own + d]
    back = remote(qown.at[1], qin, q_send, q_recv, (lax.rem(tm + 1, nt), s))

    @pl.when(tm < nt - 1)
    def _():
        back.start()

    @pl.when(tm == 0)
    def _():
        qin[...] = jnp.zeros(qin.shape, jnp.float32)

    @pl.when(tm > 0)
    def _():
        back.wait_recv()

    total = jnp.zeros((SUB, cols), jnp.float32)
    for d in range(depth):
        u0 = jnp.stack([relaxed[0, d, pl.ds(i, SUB, stride=lo), :] for i in range(lo)])
        r = natural(5, own + d) + qin[d] - u0
        put(resid.at[0], d, r)
        total = total + jnp.sum(r * r, axis=0)

    @pl.when(tm < nt - 1)
    def _():
        back.wait_send()

    parts[0] = total
    sends = []
    for i in range(1, ns):
        copy = remote(parts.at[0], allsp.at[s], n_send.at[0, i], n_recv.at[0, s],
                      (tm, lax.rem(s + i, ns)))
        copy.start()
        sends.append(copy)
    allsp[s] = total
    for i in range(1, ns):
        q = lax.rem(s + i, ns)
        remote(parts.at[0], allsp.at[q], n_send.at[0, i], n_recv.at[0, q], (tm, q)).wait_recv()
    total = allsp[0]
    for q in range(1, ns):
        total = total + allsp[q]
    parts[1] = total
    for i in range(1, nt):
        copy = remote(parts.at[1], alltm.at[tm], n_send.at[1, i], n_recv.at[1, tm],
                      (lax.rem(tm + i, nt), s))
        copy.start()
        sends.append(copy)
    alltm[tm] = total
    for i in range(1, nt):
        q = lax.rem(tm + i, nt)
        remote(parts.at[1], alltm.at[q], n_send.at[1, i], n_recv.at[1, q], (q, s)).wait_recv()
    total = alltm[0]
    for q in range(1, nt):
        total = total + alltm[q]
    norm[...] = jnp.full(norm.shape, jnp.sum(total), jnp.float32)
    for copy in sends + pending:
        copy.wait_send()


def local(nt, ns, state, source, absorption):
    depth, rows, cols = absorption.shape
    lo = rows // SUB
    layers = ns * depth
    others = ns // 2 - 1
    fields = CF + 2
    f32 = jnp.float32
    dma = pltpu.SemaphoreType.DMA
    big = max(ns, nt)
    relaxed, resid, norm = pl.pallas_call(
        functools.partial(kernel, nt, ns),
        out_shape=(
            jax.ShapeDtypeStruct(source.shape, f32),
            jax.ShapeDtypeStruct((1,) + absorption.shape, f32),
            jax.ShapeDtypeStruct((SUB, cols), f32),
        ),
        in_specs=[pl.BlockSpec(memory_space=pl.ANY)] * 3,
        out_specs=[pl.BlockSpec(memory_space=pltpu.VMEM)] * 3,
        scratch_shapes=[
            pltpu.VMEM((fields, layers, rows, cols), f32),
            pltpu.VMEM((layers, lo, SUB, cols), f32),
            pltpu.VMEM((layers + 2, lo, SUB, cols), f32),
            pltpu.VMEM((layers, lo, SUB, cols), f32),
            pltpu.VMEM((layers, lo, SUB, cols), f32),
            pltpu.VMEM((layers, lo, SUB, cols), f32),
            pltpu.VMEM((2, depth, lo, SUB, cols), f32),
            pltpu.VMEM((depth, lo, SUB, cols), f32),
            pltpu.VMEM((SUB, cols), f32),
            pltpu.VMEM((ns, SUB, cols), f32),
            pltpu.VMEM((nt, SUB, cols), f32),
            pltpu.VMEM((2, SUB, cols), f32),
            dma((fields,)),
            dma((fields, 1 + 2 * others)),
            dma((fields, ns)),
            dma((depth, 1 + 2 * others)),
            dma((depth, ns)),
            dma((depth,)),
            dma,
            dma,
            dma((2, big)),
            dma((2, big)),
        ],
        compiler_params=pltpu.CompilerParams(
            collective_id=0, has_side_effects=True, vmem_limit_bytes=48 * 1024 * 1024
        ),
        name="fcf",
    )(state, source, absorption)
    return relaxed, resid, norm[0, 0]


def solution(mesh):
    nt, ns = mesh.shape["tm"], mesh.shape["space"]
    return jax.shard_map(
        functools.partial(local, nt, ns),
        mesh=mesh,
        in_specs=(
            P("tm", "space", None, None),
            P("tm", "space", None, None),
            P("space", None, None),
        ),
        out_specs=(P("tm", "space", None, None), P("tm", "space", None, None), P()),
        check_vma=False,
    )
```

time: 142 us -> 68.9 us (0.49)
  Pallas kernels: 0 us -> 63.1 us
  blocking collectives: 55.8 us -> 0 us
  waiting for transfers between devices: 37.7 us -> 0 us
  other arithmetic: 24.6 us -> 0 us
  between operations: 14.3 us -> 0.65 us
  starting transfers between devices: 7.81 us -> 0 us
  local copies, waits for them, and re-layouts: 0.94 us -> 4.94 us
    pallas_call x0 -> x1, Pallas kernels: none -> 63.1 us  [local(): pl.pallas_call(functools.partial(kernel, nt, ns), out_shape=(jax.ShapeDty...]
    psum x1 -> x0, blocking collectives: 42.3 us -> none  [local(): lax.psum(jnp.sum(coarse_residual * coarse_residual), ('tm', 'space'))]
    all_gather x1 -> x0, waiting for transfers between devices: 31.4 us -> none  [local(): gathered = lax.all_gather(stacked, 'space', axis=1, tiled=True)]
    add x31 -> x0, other arithmetic: 14.3 us -> none  [the longest x30 14.2 us: step_whole(): field + weight * (rhs - apply_inner(extended, diag_full)) / diag_full]
    all_gather x2 -> x0, blocking collectives: 13.5 us -> none  [back_full(): lax.all_gather(previous(own_layers(last)), 'space', axis=0, tiled=True)]
    ppermute x2 -> x0, starting transfers between devices: 7.77 us -> none  [shifted(): return lax.ppermute(value, axis, pairs)]
    ppermute x2 -> x0, waiting for transfers between devices: 6.35 us -> none  [shifted(): return lax.ppermute(value, axis, pairs)]
    unnamed x2 -> x8, local copies, waits for them, and re-layouts: 0.01 us -> 4.43 us
  transfers between devices with their start and end apart: 3 -> 0, of which waited for: 3 -> 0; matrix products, arithmetic and copies ran while one was open for 0% -> 0% of each run, Pallas kernels for 0% -> 0%
where the time goes in v1:
time: 68.9 us; the launch traced here: 68.7 us
  Pallas kernels  63.1 us (92%)
  local copies, waits for them, and re-layouts  4.94 us (7%)
    pallas_call x1, Pallas kernels, local(): pl.pallas_call(functools.partial(kernel, nt, ns), out_shape=(jax.ShapeDty...  63.1 us
    unnamed x8, local copies, waits for them, and re-layouts  4.43 us

profile of v1, /device:TPU:0, one launch (start us, length us, event | category | flops | bytes accessed | tf_op | source)
XLA Modules:
  0.0 68.7 jit_solution(4752699987858081669)
XLA Ops:
  0.6 0.0 copy-start
  0.6 1.0 %copy-done = f32[4,4,64,128]{3,2,1,0:T(8,128)S(1)} copy-done((f32[4,4,64,128]{3,2,1,0:T(8,128)S(1)}, f32[4,4,64,128]{3,2,1,0:T(8,128)}, u32[]{:S(2)}) %copy-start) | copy-done | bytes 524312
  1.7 0.0 copy-start.1
  1.7 1.0 %copy-done.1 = f32[4,4,64,128]{3,2,1,0:T(8,128)S(1)} copy-done((f32[4,4,64,128]{3,2,1,0:T(8,128)S(1)}, f32[4,4,64,128]{3,2,1,0:T(8,128)}, u32[]{:S(2)}) %copy-start.1) | copy-done | bytes 524312
  2.7 0.0 copy-start.2
  2.7 0.9 %copy-done.2 = f32[4,64,128]{2,1,0:T(8,128)S(1)} copy-done((f32[4,64,128]{2,1,0:T(8,128)S(1)}, f32[4,64,128]{2,1,0:T(8,128)}, u32[]{:S(2)}) %copy-start.2) | copy-done | bytes 131096
  3.6 63.1 %fcf.1 = (f32[4,4,64,128]{3,2,1,0:T(8,128)S(1)}, f32[1,4,64,128]{3,2,1,0:T(8,128)S(1)}, f32[8,128]{1,0:T(8,128)S(1)}) custom-call(f32[4,4,64,128]{3,2,1,0:T(8,128)S(1)} %copy-done, f32[4,4,64,128]{3,2,1,0:T(8,128)S(1)} %copy-done.1, f32[4,64,128]{2,1,0:T(8,128)S(1)} %copy-done.2), custom_call_target="tpu_custom_call" | custom-call | tf_op jit(solution)/shard_map/fcf/pallas_call | solution.py:313
  66.7 0.5 slice.3
  67.2 0.8 %copy.8 = f32[4,4,64,128]{3,2,1,0:T(8,128)} copy(f32[4,4,64,128]{3,2,1,0:T(8,128)S(1)} %get-tuple-element.12) | data formatting | bytes 1048576
  68.0 0.7 copy.9
Async XLA Ops:
  0.6 1.0 %copy-start = (f32[4,4,64,128]{3,2,1,0:T(8,128)S(1)}, f32[4,4,64,128]{3,2,1,0:T(8,128)}, u32[]{:S(2)}) copy-start(f32[4,4,64,128]{3,2,1,0:T(8,128)} %state.1) | copy-start | bytes 1572868
  1.7 1.0 %copy-start.1 = (f32[4,4,64,128]{3,2,1,0:T(8,128)S(1)}, f32[4,4,64,128]{3,2,1,0:T(8,128)}, u32[]{:S(2)}) copy-start(f32[4,4,64,128]{3,2,1,0:T(8,128)} %source.1) | copy-start | bytes 1572868
  2.7 0.9 %copy-start.2 = (f32[4,64,128]{2,1,0:T(8,128)S(1)}, f32[4,64,128]{2,1,0:T(8,128)}, u32[]{:S(2)}) copy-start(f32[4,64,128]{2,1,0:T(8,128)} %absorb.1) | copy-start | bytes 393220

commit v2 on v1

--- a/solution.py
+++ b/solution.py
@@ -29,10 +29,10 @@
     return float(c[0]), float(c[2]), float(c[4])
 
 
-def kernel(nt, ns, state, source, absorb, relaxed, resid, norm,
-           nat, c4, work, held, full, pfull, qown, qin, tot, allsp, alltm, parts,
+def kernel(nt, ns, state, source, absorb, relaxed_out, resid_out, norm,
+           relaxed, resid, nat, c4, work, held, full, pfull, qown, qin, tot, allsp, alltm, parts,
            loc_sem, g_send, g_recv, p_send, p_recv, sh_send, q_send, q_recv,
-           n_send, n_recv):
+           n_send, n_recv, o_sem):
     tm = lax.axis_index("tm")
     s = lax.axis_index("space")
     depth, rows, cols = absorb.shape
@@ -73,9 +73,11 @@
         pending.append(copy)
 
     for f in range(fields):
+        here = quarter(f, s)
+        loads[f].wait()
         for i, chip in enumerate(chips):
-            go(remote(srcs[f], quarter(f, s), g_send.at[f, 1 + i], g_recv.at[f, s], (tm, chip)))
-        go(remote(srcs[f], quarter(f, s), g_send.at[f, 0], g_recv.at[f, s], (tm, partner)))
+            go(remote(here, here, g_send.at[f, 1 + i], g_recv.at[f, s], (tm, chip)))
+        go(remote(here, here, g_send.at[f, 0], g_recv.at[f, s], (tm, partner)))
 
     def relay(f):
         for i, chip in enumerate(chips):
@@ -83,9 +85,7 @@
             remote(here, here, g_send.at[f, 0], g_recv.at[f, chip], (tm, partner)).wait_recv()
             go(remote(here, here, g_send.at[f, 1 + others + i], g_recv.at[f, chip], (tm, partner)))
 
-    def arrive(f, mine=True):
-        if mine:
-            loads[f].wait()
+    def arrive(f):
         there = [partner] + [lax.rem(partner + 2 * i, ns) for i in range(1, others + 1)]
         for q in there:
             here = quarter(f, q)
@@ -108,16 +108,13 @@
         right = pltpu.roll(flat, cols - 1, 1).reshape(v.shape)
         return total + jnp.where(first_lane, 0.0, left) + jnp.where(last_lane, 0.0, right)
 
-    def sweep(finish, unroll=4):
-        def body(i, carry):
-            before, now = carry
-            for j in range(unroll):
-                z = i * unroll + j
-                after = work[z + 2]
-                finish(z, c4[z] * (before + after + beside(now)), now)
-                before, now = now, after
-            return before, now
-        lax.fori_loop(0, layers // unroll, body, (work[0], work[1]))
+    def sweep(finish, start=0, count=None):
+        before, now = work[start], work[start + 1]
+        for j in range(layers if count is None else count):
+            z = start + j
+            after = work[z + 2]
+            finish(z, c4[z] * (before + after + beside(now)), now)
+            before, now = now, after
 
     def plain(z, moved, now):
         work[z + 1] = moved
@@ -132,12 +129,15 @@
         work[z + 1] = h
         held[z] = h
 
-    def phi(finish):
-        sweep(plain)
-        sweep(adding(r1 / r2))
-        sweep(plain)
-        sweep(adding(r0 / r2))
-        sweep(finish)
+    def phi(finish, mine=False):
+        steps = [plain, adding(r1 / r2), plain, adding(r0 / r2), finish]
+        for k, step in enumerate(steps):
+            margin = len(steps) - 1 - k
+            count = depth + 2 * margin
+            if mine and count < layers:
+                sweep(step, jnp.clip(own - margin, 0, layers - count), count)
+            else:
+                sweep(step)
 
     def each_layer(do):
         def body(z, _):
@@ -175,10 +175,9 @@
     relay(4)
     arrive(3)
     phi(onward(3))
-    phi(to_full)
+    phi(to_full, mine=True)
     relay(5)
 
-    loads[4].wait()
     chunk = lambda d: pl.ds(own + d, 1)
     for d in range(depth):
         qown[0, d] = full[own + d] + natural(4, own + d)
@@ -228,12 +227,17 @@
         for shift in shifts:
             shift.wait_send()
 
-    arrive(4, mine=False)
+    arrive(4)
     arrive(5)
+
+    outs = []
 
     def save(j):
         for d in range(depth):
             put(relaxed.at[j], d, full[own + d])
+        out = pltpu.make_async_copy(relaxed.at[j], relaxed_out.at[j], o_sem.at[j])
+        out.start()
+        outs.append(out)
 
     each_layer(lambda z: start_with(z, pfull[z]))
     phi(onward(5))
@@ -241,7 +245,7 @@
     for j in range(1, CF):
         phi(onward(1 + j))
         save(j)
-    phi(to_full)
+    phi(to_full, mine=True)
     for d in range(depth):
         qown[1, d] = full[own + d]
     back = remote(qown.at[1], qin, q_send, q_recv, (lax.rem(tm + 1, nt), s))
@@ -269,6 +273,9 @@
     def _():
         back.wait_send()
 
+    out = pltpu.make_async_copy(resid, resid_out, o_sem.at[CF])
+    out.start()
+    outs.append(out)
     parts[0] = total
     sends = []
     for i in range(1, ns):
@@ -296,9 +303,11 @@
     total = alltm[0]
     for q in range(1, nt):
         total = total + alltm[q]
-    norm[...] = jnp.full(norm.shape, jnp.sum(total), jnp.float32)
+    norm[0] = jnp.sum(total)
     for copy in sends + pending:
         copy.wait_send()
+    for out in outs:
+        out.wait()
 
 
 def local(nt, ns, state, source, absorption):
@@ -315,11 +324,14 @@
         out_shape=(
             jax.ShapeDtypeStruct(source.shape, f32),
             jax.ShapeDtypeStruct((1,) + absorption.shape, f32),
-            jax.ShapeDtypeStruct((SUB, cols), f32),
+            jax.ShapeDtypeStruct((1,), f32),
         ),
-        in_specs=[pl.BlockSpec(memory_space=pl.ANY)] * 3,
-        out_specs=[pl.BlockSpec(memory_space=pltpu.VMEM)] * 3,
+        in_specs=[pl.BlockSpec(memory_space=pltpu.HBM)] * 3,
+        out_specs=[pl.BlockSpec(memory_space=pltpu.HBM)] * 2
+        + [pl.BlockSpec(memory_space=pltpu.SMEM)],
         scratch_shapes=[
+            pltpu.VMEM(source.shape, f32),
+            pltpu.VMEM((1,) + absorption.shape, f32),
             pltpu.VMEM((fields, layers, rows, cols), f32),
             pltpu.VMEM((layers, lo, SUB, cols), f32),
             pltpu.VMEM((layers + 2, lo, SUB, cols), f32),
@@ -342,13 +354,14 @@
             dma,
             dma((2, big)),
             dma((2, big)),
+            dma((CF + 1,)),
         ],
         compiler_params=pltpu.CompilerParams(
-            collective_id=0, has_side_effects=True, vmem_limit_bytes=48 * 1024 * 1024
+            collective_id=0, has_side_effects=True, vmem_limit_bytes=60 * 1024 * 1024
         ),
         name="fcf",
     )(state, source, absorption)
-    return relaxed, resid, norm[0, 0]
+    return relaxed, resid, norm.reshape(())
 
 
 def solution(mesh):

time: 68.9 us -> 58.6 us (0.85)
  Pallas kernels: 63.1 us -> 53.5 us
  local copies, waits for them, and re-layouts: 4.94 us -> 2.58 us
  between operations: 0.65 us -> 2.41 us
    pallas_call x1, Pallas kernels: 63.1 us -> 53.5 us  [local(): pl.pallas_call(functools.partial(kernel, nt, ns), out_shape=(jax.ShapeDty...]
    unnamed x8 -> x4, local copies, waits for them, and re-layouts: 4.43 us -> 2.58 us
where the time goes in v2:
time: 58.6 us; the launch traced here: 58.5 us
  Pallas kernels  53.5 us (91%)
  local copies, waits for them, and re-layouts  2.58 us (4%)
  between operations  2.41 us (4%)
    pallas_call x1, Pallas kernels, local(): pl.pallas_call(functools.partial(kernel, nt, ns), out_shape=(jax.ShapeDty...  53.5 us
    unnamed x4, local copies, waits for them, and re-layouts  2.58 us

profile of v2, /device:TPU:0, one launch (start us, length us, event | category | flops | bytes accessed | tf_op | source)
XLA Modules:
  0.0 58.5 jit_solution(11537225400418428942)
XLA Ops:
  0.6 53.5 %fcf.1 = (f32[4,4,64,128]{3,2,1,0:T(8,128)}, f32[1,4,64,128]{3,2,1,0:T(8,128)}, f32[1]{0:T(128)}) custom-call(f32[4,4,64,128]{3,2,1,0:T(8,128)} %state.1, f32[4,4,64,128]{3,2,1,0:T(8,128)} %source.1, f32[4,64,128]{2,1,0:T(8,128)} %absorb.1), custom_call_target="tpu_custom_call" | custom-call | tf_op jit(solution)/shard_map/fcf/pallas_call | solution.py:322
  54.1 0.0 copy-start
  54.1 1.9 %copy.9 = f32[4,4,64,128]{3,2,1,0:T(8,128)} copy(f32[4,4,64,128]{3,2,1,0:T(8,128)} %get-tuple-element.12) | data formatting | bytes 1048576
  56.0 0.0 copy-done
  56.1 0.7 %copy.10 = f32[1,4,64,128]{3,2,1,0:T(8,128)} copy(f32[1,4,64,128]{3,2,1,0:T(8,128)S(1)} %copy-done) | data formatting | bytes 262144
Async XLA Ops:
  54.1 1.9 %copy-start = (f32[1,4,64,128]{3,2,1,0:T(8,128)S(1)}, f32[1,4,64,128]{3,2,1,0:T(8,128)}, u32[]{:S(2)}) copy-start(f32[1,4,64,128]{3,2,1,0:T(8,128)} %get-tuple-element.13) | copy-start | bytes 393220

commit v3 on v2

--- a/solution.py
+++ b/solution.py
@@ -30,8 +30,8 @@
 
 
 def kernel(nt, ns, state, source, absorb, relaxed_out, resid_out, norm,
-           relaxed, resid, nat, c4, work, held, full, pfull, qown, qin, tot, allsp, alltm, parts,
-           loc_sem, g_send, g_recv, p_send, p_recv, sh_send, q_send, q_recv,
+           relaxed, resid, nat, c4, work, held, full, pfull, qown, qin, eown, ein, tot, allsp, alltm, parts,
+           loc_sem, g_send, g_recv, p_send, p_recv, sh_send, q_send, q_recv, e_send, e_recv,
            n_send, n_recv, o_sem):
     tm = lax.axis_index("tm")
     s = lax.axis_index("space")
@@ -67,17 +67,23 @@
             device_id=where, device_id_type=MESH)
 
     pending = []
+    late = CF
 
     def go(copy):
         copy.start()
         pending.append(copy)
 
-    for f in range(fields):
+    def spread(f):
         here = quarter(f, s)
-        loads[f].wait()
+        if f != late:
+            loads[f].wait()
         for i, chip in enumerate(chips):
             go(remote(here, here, g_send.at[f, 1 + i], g_recv.at[f, s], (tm, chip)))
         go(remote(here, here, g_send.at[f, 0], g_recv.at[f, s], (tm, partner)))
+
+    for f in range(fields):
+        if f != late:
+            spread(f)
 
     def relay(f):
         for i, chip in enumerate(chips):
@@ -172,15 +178,16 @@
     relay(3)
     arrive(2)
     phi(onward(2))
-    relay(4)
     arrive(3)
     phi(onward(3))
     phi(to_full, mine=True)
     relay(5)
 
+    loads[late].wait()
+
     chunk = lambda d: pl.ds(own + d, 1)
     for d in range(depth):
-        qown[0, d] = full[own + d] + natural(4, own + d)
+        qown[0, d] = full[own + d] + natural(late, own + d)
     shifts = [remote(qown.at[0, pl.ds(d, 1)], pfull.at[chunk(d)], sh_send.at[d], p_recv.at[d, s],
                      (lax.rem(tm + 1, nt), s)) for d in range(depth)]
 
@@ -227,7 +234,7 @@
         for shift in shifts:
             shift.wait_send()
 
-    arrive(4)
+    spread(late)
     arrive(5)
 
     outs = []
@@ -242,7 +249,18 @@
     each_layer(lambda z: start_with(z, pfull[z]))
     phi(onward(5))
     save(0)
+    for d in range(depth):
+        eown[d] = natural(5, own + d) - full[own + d]
+    rest = remote(eown, ein, e_send, e_recv, (lax.rem(tm + nt - 1, nt), s))
+
+    @pl.when(tm > 0)
+    def _():
+        rest.start()
+
     for j in range(1, CF):
+        if 1 + j == late:
+            relay(late)
+            arrive(late)
         phi(onward(1 + j))
         save(j)
     phi(to_full, mine=True)
@@ -254,28 +272,22 @@
     def _():
         back.start()
 
+    def squares(value):
+        return jnp.sum(value * value, axis=(0, 1))
+
+    tot[...] = jnp.zeros(tot.shape, jnp.float32)
+
     @pl.when(tm == 0)
     def _():
         qin[...] = jnp.zeros(qin.shape, jnp.float32)
-
-    @pl.when(tm > 0)
-    def _():
-        back.wait_recv()
-
-    total = jnp.zeros((SUB, cols), jnp.float32)
-    for d in range(depth):
-        u0 = jnp.stack([relaxed[0, d, pl.ds(i, SUB, stride=lo), :] for i in range(lo)])
-        r = natural(5, own + d) + qin[d] - u0
-        put(resid.at[0], d, r)
-        total = total + jnp.sum(r * r, axis=0)
+        tot[...] = squares(eown[...])
 
     @pl.when(tm < nt - 1)
     def _():
-        back.wait_send()
-
-    out = pltpu.make_async_copy(resid, resid_out, o_sem.at[CF])
-    out.start()
-    outs.append(out)
+        rest.wait_recv()
+        tot[...] = tot[...] + squares(qown[1] + ein[...])
+
+    total = tot[...]
     parts[0] = total
     sends = []
     for i in range(1, ns):
@@ -304,6 +316,25 @@
     for q in range(1, nt):
         total = total + alltm[q]
     norm[0] = jnp.sum(total)
+
+    @pl.when(tm > 0)
+    def _():
+        back.wait_recv()
+
+    for d in range(depth):
+        put(resid.at[0], d, qin[d] + eown[d])
+    out = pltpu.make_async_copy(resid, resid_out, o_sem.at[CF])
+    out.start()
+    outs.append(out)
+
+    @pl.when(tm < nt - 1)
+    def _():
+        back.wait_send()
+
+    @pl.when(tm > 0)
+    def _():
+        rest.wait_send()
+
     for copy in sends + pending:
         copy.wait_send()
     for out in outs:
@@ -340,6 +371,8 @@
             pltpu.VMEM((layers, lo, SUB, cols), f32),
             pltpu.VMEM((2, depth, lo, SUB, cols), f32),
             pltpu.VMEM((depth, lo, SUB, cols), f32),
+            pltpu.VMEM((depth, lo, SUB, cols), f32),
+            pltpu.VMEM((depth, lo, SUB, cols), f32),
             pltpu.VMEM((SUB, cols), f32),
             pltpu.VMEM((ns, SUB, cols), f32),
             pltpu.VMEM((nt, SUB, cols), f32),
@@ -350,6 +383,8 @@
             dma((depth, 1 + 2 * others)),
             dma((depth, ns)),
             dma((depth,)),
+            dma,
+            dma,
             dma,
             dma,
             dma((2, big)),

time: 58.6 us -> 54.4 us (0.928)
  Pallas kernels: 53.5 us -> 49.3 us
    pallas_call x1, Pallas kernels: 53.5 us -> 49.3 us  [local(): pl.pallas_call(functools.partial(kernel, nt, ns), out_shape=(jax.ShapeDty...]
where the time goes in v3:
time: 54.4 us; the launch traced here: 54.3 us
  Pallas kernels  49.3 us (91%)
  local copies, waits for them, and re-layouts  2.58 us (5%)
  between operations  2.41 us (4%)
    pallas_call x1, Pallas kernels, local(): pl.pallas_call(functools.partial(kernel, nt, ns), out_shape=(jax.ShapeDty...  49.3 us
    unnamed x4, local copies, waits for them, and re-layouts  2.58 us

profile of v3, /device:TPU:0, one launch (start us, length us, event | category | flops | bytes accessed | tf_op | source)
XLA Modules:
  0.0 54.3 jit_solution(16419602781123044819)
XLA Ops:
  0.6 49.3 %fcf.1 = (f32[4,4,64,128]{3,2,1,0:T(8,128)}, f32[1,4,64,128]{3,2,1,0:T(8,128)}, f32[1]{0:T(128)}) custom-call(f32[4,4,64,128]{3,2,1,0:T(8,128)} %state.1, f32[4,4,64,128]{3,2,1,0:T(8,128)} %source.1, f32[4,64,128]{2,1,0:T(8,128)} %absorb.1), custom_call_target="tpu_custom_call" | custom-call | tf_op jit(solution)/shard_map/fcf/pallas_call | solution.py:353
  49.9 0.0 copy-start
  49.9 1.9 %copy.9 = f32[4,4,64,128]{3,2,1,0:T(8,128)} copy(f32[4,4,64,128]{3,2,1,0:T(8,128)} %get-tuple-element.12) | data formatting | bytes 1048576
  51.9 0.0 copy-done
  51.9 0.7 %copy.10 = f32[1,4,64,128]{3,2,1,0:T(8,128)} copy(f32[1,4,64,128]{3,2,1,0:T(8,128)S(1)} %copy-done) | data formatting | bytes 262144
Async XLA Ops:
  49.9 1.9 %copy-start = (f32[1,4,64,128]{3,2,1,0:T(8,128)S(1)}, f32[1,4,64,128]{3,2,1,0:T(8,128)}, u32[]{:S(2)}) copy-start(f32[1,4,64,128]{3,2,1,0:T(8,128)} %get-tuple-element.13) | copy-start | bytes 393220
